TPU v7x, 32 devices: a whole 2x2x4 slice. The times are simulated.
32 devices in a mesh: section: 4 (over y, x), fsdp: 8 (over z, core).
Axes of the slice: x: 2, y: 2, z: 4, core: 2. Of those that a mesh axis runs over, the one named last changes fastest.
Arguments:
- patches: bfloat16 [8, 1024, 768], P(None, 'fsdp'), may hold values from -6 to 6
- cotangent: bfloat16 [8, 1024, 768], P(None, 'fsdp'), may hold values from -6 to 6
- embed_blocks: int32 [8], replicated, may hold values from 4 to 6
- ratio_index: int32 [8], replicated, may hold values from 0 to 2
- depth: int32 [8], replicated, may hold values from 2 to 4
- w_up: bfloat16 [4, 768, 3072], P('section', 'fsdp'), may hold values from -0.21875 to 0.21875
- w_down: bfloat16 [4, 3072, 768], P('section', 'fsdp'), may hold values from -0.109375 to 0.109375
- ln_gain: bfloat16 [4, 768], P('section', 'fsdp'), may hold values from 0.099609375 to 1.8984375
Outputs:
- grad_up: float32 [4, 768, 3072], P('section', 'fsdp')
- grad_down: float32 [4, 3072, 768], P('section', 'fsdp')
- grad_gain: float32 [4, 768], P('section', 'fsdp')
All inputs are finite; a program needn't handle non-finite values.
Results may differ from a plain program's by a relative error of at most 0.028.
Values may be sent and summed in bfloat16 or wider, within the bound.
A program may use at most 192 MiB of HBM per device.

v0:
```python
import jax
import jax.numpy as jnp
from jax import lax
from jax.sharding import PartitionSpec as P

BLOCK = 128


EPSILON = 1e-05


def passed_along(block, axis, distance):
    devices = range(lax.axis_size(axis))
    route = [(i - distance, i) for i in devices if i - distance in devices]
    return lax.ppermute(block, axis, route)


def micro_masks(blocks, ratio, feature_count, hidden_count):
    width_int = blocks * BLOCK
    hidden_int = width_int * (6 + ratio) // 2
    embed_mask = (lax.iota(jnp.int32, feature_count) < width_int).astype(jnp.float32)
    hidden_mask = (lax.iota(jnp.int32, hidden_count) < hidden_int).astype(jnp.float32)
    return (embed_mask, hidden_mask, width_int.astype(jnp.float32))


def layer_norm(inputs, embed_mask, width_float):
    values = inputs.astype(jnp.float32) * embed_mask
    center_value = jnp.sum(values, axis=-1, keepdims=True) / width_float
    centered = (values - center_value) * embed_mask
    variance = jnp.sum(centered * centered, axis=-1, keepdims=True) / width_float
    inv_std = lax.rsqrt(variance + EPSILON)
    return (centered * inv_std, inv_std)


def layer_forward(
    inputs, gain_vector, weight_up, weight_down, embed_mask, hidden_mask, active, width_float
):
    standard, inv_std = layer_norm(inputs, embed_mask, width_float)
    normed = (standard * gain_vector.astype(jnp.float32)).astype(jnp.bfloat16)
    hidden = jnp.dot(normed, weight_up, preferred_element_type=jnp.float32)
    activated = (jax.nn.gelu(hidden) * hidden_mask).astype(jnp.bfloat16)
    branch = jnp.dot(activated, weight_down, preferred_element_type=jnp.float32)
    output = (inputs.astype(jnp.float32) + active * embed_mask * branch).astype(jnp.bfloat16)
    return (output, hidden)


def layer_backward(
    inputs,
    hidden,
    grad_out,
    gain_vector,
    weight_up,
    weight_down,
    embed_mask,
    hidden_mask,
    active,
    width_float,
):
    standard, inv_std = layer_norm(inputs, embed_mask, width_float)
    gain_float = gain_vector.astype(jnp.float32)
    normed = (standard * gain_float).astype(jnp.bfloat16)
    activated = (jax.nn.gelu(hidden) * hidden_mask).astype(jnp.bfloat16)
    grad_branch = (active * embed_mask * grad_out.astype(jnp.float32)).astype(jnp.bfloat16)
    grad_act = lax.dot_general(
        grad_branch, weight_down, (((1,), (1,)), ((), ())), preferred_element_type=jnp.float32
    )
    unused, pullback = jax.vjp(jax.nn.gelu, hidden)
    grad_hidden = pullback(grad_act * hidden_mask)[0].astype(jnp.bfloat16)
    grad_normed = lax.dot_general(
        grad_hidden, weight_up, (((1,), (1,)), ((), ())), preferred_element_type=jnp.float32
    )
    grad_standard = grad_normed * gain_float * embed_mask
    grad_gain = jnp.sum(grad_normed * standard, axis=0)
    first_mean = jnp.sum(grad_standard, axis=-1, keepdims=True) / width_float
    second_mean = jnp.sum(grad_standard * standard, axis=-1, keepdims=True) / width_float
    grad_norm_in = inv_std * (grad_standard - first_mean * embed_mask - standard * second_mean)
    grad_in = (grad_out.astype(jnp.float32) + grad_norm_in).astype(jnp.bfloat16)
    return (grad_in, normed, grad_hidden, activated, grad_branch, grad_gain)


def contract_rows(left, right):
    return lax.dot_general(
        left, right, (((0,), (0,)), ((), ())), preferred_element_type=jnp.float32
    )


def store_row(stash, value, slot, is_valid):
    row = jnp.where(is_valid, value, stash[slot])
    return lax.dynamic_update_index_in_dim(stash, row, slot, 0)


def per_device(patches, cotangent, embed_blocks, ratio_index, depth, w_up, w_down, ln_gain):
    section_count = lax.axis_size("section")
    section_index = lax.axis_index("section")
    gathered_up, gathered_down, gathered_gain = (
        lax.all_gather(w_up, "fsdp", axis=1, tiled=True),
        lax.all_gather(w_down, "fsdp", axis=1, tiled=True),
        lax.all_gather(ln_gain, "fsdp", axis=1, tiled=True),
    )
    weight_up = gathered_up[0]
    weight_down = gathered_down[0]
    gain_vector = gathered_gain[0]
    feature_count, hidden_count = weight_up.shape
    micro_count = patches.shape[0]
    row_count = patches.shape[1]
    tick_total = micro_count + section_count - 1

    def masks_of(micro_index):
        is_valid = jnp.logical_and(micro_index >= 0, micro_index < micro_count)
        safe_index = jnp.clip(micro_index, 0, micro_count - 1)
        embed_mask, hidden_mask, width_float = micro_masks(
            embed_blocks[safe_index], ratio_index[safe_index], feature_count, hidden_count
        )
        active = (section_index < depth[safe_index]).astype(jnp.float32)
        return (safe_index, is_valid, embed_mask, hidden_mask, active, width_float, is_valid)

    def forward_tick(tick_count, carry):
        incoming, stash_in, stash_hidden = carry
        safe_index, is_valid, embed_mask, hidden_mask, active, width_float, should_run = masks_of(
            tick_count - section_index
        )
        first_in = (patches[safe_index].astype(jnp.float32) * embed_mask).astype(jnp.bfloat16)
        inputs = jnp.where(section_index == 0, first_in, incoming)

        def forward_compute(values):
            return layer_forward(
                values,
                gain_vector,
                weight_up,
                weight_down,
                embed_mask,
                hidden_mask,
                active,
                width_float,
            )

        def forward_bypass(values):
            return (values, jnp.zeros((row_count, hidden_count), jnp.float32))

        output, hidden = lax.cond(should_run, forward_compute, forward_bypass, inputs)
        stash_in = store_row(stash_in, inputs, safe_index, is_valid)
        stash_hidden = store_row(stash_hidden, hidden, safe_index, is_valid)
        sent = passed_along(output, "section", 1)
        return (sent, stash_in, stash_hidden)

    start_carry = (
        jnp.zeros((row_count, feature_count), jnp.bfloat16),
        jnp.zeros((micro_count, row_count, feature_count), jnp.bfloat16),
        jnp.zeros((micro_count, row_count, hidden_count), jnp.float32),
    )
    unused_last, stash_in, stash_hidden = lax.fori_loop(0, tick_total, forward_tick, start_carry)
    extra_start = (
        jnp.zeros((micro_count, row_count, feature_count), jnp.bfloat16),
        jnp.zeros((micro_count, row_count, hidden_count), jnp.bfloat16),
    )

    def backward_tick(tick_count, carry):
        incoming, acc_down, acc_gain, extra = carry
        safe_index, is_valid, embed_mask, hidden_mask, active, width_float, should_run = masks_of(
            tick_count - (section_count - 1 - section_index)
        )
        last_in = (cotangent[safe_index].astype(jnp.float32) * embed_mask).astype(jnp.bfloat16)
        grad_out = jnp.where(section_index == section_count - 1, last_in, incoming)

        def backward_compute(operands):
            values, hidden_values, grad_values = operands
            grad_in, normed, grad_hidden, activated, grad_branch, grad_gain = layer_backward(
                values,
                hidden_values,
                grad_values,
                gain_vector,
                weight_up,
                weight_down,
                embed_mask,
                hidden_mask,
                active,
                width_float,
            )
            term_down = contract_rows(activated, grad_branch)
            term_extra = (normed, grad_hidden)
            return (grad_in, term_down, grad_gain, term_extra)

        def backward_bypass(operands):
            term_extra = (
                jnp.zeros((row_count, feature_count), jnp.bfloat16),
                jnp.zeros((row_count, hidden_count), jnp.bfloat16),
            )
            return (
                operands[2],
                jnp.zeros((hidden_count, feature_count), jnp.float32),
                jnp.zeros((feature_count,), jnp.float32),
                term_extra,
            )

        grad_in, term_down, term_gain, term_extra = lax.cond(
            should_run,
            backward_compute,
            backward_bypass,
            (stash_in[safe_index], stash_hidden[safe_index], grad_out),
        )
        acc_down = acc_down + term_down
        acc_gain = acc_gain + term_gain
        extra = (
            store_row(extra[0], term_extra[0], safe_index, is_valid),
            store_row(extra[1], term_extra[1], safe_index, is_valid),
        )
        sent = passed_along(grad_in, "section", -1)
        return (sent, acc_down, acc_gain, extra)

    back_carry = (
        jnp.zeros((row_count, feature_count), jnp.bfloat16),
        jnp.zeros((hidden_count, feature_count), jnp.float32),
        jnp.zeros((feature_count,), jnp.float32),
        extra_start,
    )
    unused_first, acc_down, acc_gain, extra = lax.fori_loop(
        0, tick_total, backward_tick, back_carry
    )
    flat_normed = extra[0].reshape(micro_count * row_count, feature_count)
    flat_grad = extra[1].reshape(micro_count * row_count, hidden_count)
    part_up = lax.psum_scatter(
        contract_rows(flat_normed, flat_grad).astype(jnp.bfloat16),
        "fsdp",
        scatter_dimension=0,
        tiled=True,
    ).astype(jnp.float32)
    grad_up = part_up[None]
    grad_down, grad_gain = (
        lax.psum_scatter(
            acc_down[None].astype(jnp.bfloat16), "fsdp", scatter_dimension=1, tiled=True
        ).astype(jnp.float32),
        lax.psum_scatter(
            acc_gain[None].astype(jnp.bfloat16), "fsdp", scatter_dimension=1, tiled=True
        ).astype(jnp.float32),
    )
    return (grad_up, grad_down, grad_gain)


def solution(mesh):
    return jax.shard_map(
        per_device,
        mesh=mesh,
        in_specs=(
            P(None, "fsdp", None),
            P(None, "fsdp", None),
            P(),
            P(),
            P(),
            P("section", "fsdp", None),
            P("section", "fsdp", None),
            P("section", "fsdp"),
        ),
        out_specs=(P("section", "fsdp", None), P("section", "fsdp", None), P("section", "fsdp")),
        check_vma=False,
    )
```

profile of v0, /device:TPU:0, one launch (start us, length us, event | category | flops | bytes accessed | tf_op | source)
XLA Modules:
  0.0 870.5 jit_solution(4272690858157247190)
XLA Ops:
  11.5 18.8 %all-reduce = bf16[768]{0:T(1024)(128)(2,1)S(1)} all-reduce(bf16[768]{0:T(1024)(128)(2,1)S(1)} %dynamic-update-slice), channel_id=1, replica_groups=mesh['section'=4,'fsdp'=8] {'fsdp'}, use_global_device_ids=true, to_apply=%add | all-reduce | flops 768 | bytes 3072 | tf_op jit(solution)/shard_map/squeeze | solution.py:102
  30.3 33.7 %all-gather.3.cloned.1.call-done = bf16[1,768,3072]{2,1,0:T(8,128)(2,1)} async-done(((bf16[1,96,3072]{2,1,0:T(8,128)(2,1)}), bf16[1,768,3072]{2,1,0:T(8,128)(2,1)}) %all-gather.3.cloned.1.call-update) | async-done | bytes 4718608 | tf_op jit(solution)/shard_map/all_gather | solution.py:96
  64.1 51.6 %all-gather.5.cloned.1.call-done = bf16[1,3072,768]{2,1,0:T(8,128)(2,1)} async-done(((bf16[1,384,768]{2,1,0:T(8,128)(2,1)}), bf16[1,3072,768]{2,1,0:T(8,128)(2,1)}) %all-gather.5.cloned.1.call-update) | async-done | bytes 4718608 | tf_op jit(solution)/shard_map/all_gather | solution.py:97
  122.4 217.9 %while.43 = (s32[]{:T(128)}, bf16[128,768]{1,0:T(8,128)(2,1)S(1)}, bf16[8,128,768]{2,1,0:T(8,128)(2,1)S(1)}, f32[8,128,3072]{2,1,0:T(8,128)}, s32[]{:T(128)}, /*...) while((s32[]{:T(128)}, bf16[128,768]{1,0:T(8,128)(2,1)S(1)}, ...), condition=%wide.region_5.6_spmd, body=%wide.region_0.5_spmd.sunk | while | flops 1214751872 | bytes 42530464 | solution.py:151
  127.3 7.5 conditional.5
  145.8 7.5 conditional.5
  166.9 7.5 conditional.5
  187.7 7.5 conditional.5
  207.6 7.5 conditional.5
  228.6 7.5 conditional.5
  249.5 7.5 conditional.5
  270.3 7.5 conditional.5
  292.6 10.2 %collective-permute-start = (bf16[128,768]{1,0:T(8,128)(2,1)S(1)}, bf16[128,768]{1,0:T(8,128)(2,1)S(1)}, u32[]{:S(2)}, u32[]{:S(2)}) collective-permute-start(bf16[128,768]{1,0:T(8,128)(2,1)S(1)} %get-tuple-element.1128), channel_id=1, source_target_pairs={{0,8},{8,16},{16,24},{1,9},{9,17},{17,25},{2,10},{10,18},{18,26},{... | collective-permute-start | bytes 589832 | tf_op jit(solution)/shard_map/while/body/eval_jaxpr/ppermute | solution.py:15
  326.9 10.3 %collective-permute-start = (bf16[128,768]{1,0:T(8,128)(2,1)S(1)}, bf16[128,768]{1,0:T(8,128)(2,1)S(1)}, u32[]{:S(2)}, u32[]{:S(2)}) collective-permute-start(bf16[128,768]{1,0:T(8,128)(2,1)S(1)} %get-tuple-element.1128), channel_id=1, source_target_pairs={{0,8},{8,16},{16,24},{1,9},{9,17},{17,25},{2,10},{10,18},{18,26},{... | collective-permute-start | bytes 589832 | tf_op jit(solution)/shard_map/while/body/eval_jaxpr/ppermute | solution.py:15
  345.1 372.6 %while.44 = (s32[]{:T(128)}, bf16[128,768]{1,0:T(8,128)(2,1)S(1)}, f32[3072,768]{1,0:T(8,128)}, f32[768]{0:T(1024)S(1)}, bf16[8,128,768]{2,1,0:T(8,128)(2,1)}, /...) while((s32[]{:T(128)}, bf16[128,768]{1,0:T(8,128)(2,1)S(1)}, ...), condition=%wide.region_14.15_spmd.clone, body=%wide.region_6.14_spmd.clone.sunk | while | flops 1834067840 | bytes 81301856 | solution.py:216
  359.7 8.4 select_add_fusion.4
  382.6 11.1 %select_add_fusion.4 = f32[3072,768]{1,0:T(8,128)} fusion(f32[3072,768]{1,0:T(8,128)} %get-tuple-element.1150, f32[3072,768]{1,0:T(8,128)} %get-tuple-element.1255, pred[]{:T(512)S(6)} %compare.23), kind=kLoop, calls=%fused_computation.106.clone.1 | loop fusion | flops 4718592 | bytes 28311552 | tf_op jit(solution)/shard_map/while/body/eval_jaxpr/add | solution.py:201
  408.2 11.1 %select_add_fusion.4 = f32[3072,768]{1,0:T(8,128)} fusion(f32[3072,768]{1,0:T(8,128)} %get-tuple-element.1150, f32[3072,768]{1,0:T(8,128)} %get-tuple-element.1255, pred[]{:T(512)S(6)} %compare.23), kind=kLoop, calls=%fused_computation.106.clone.1 | loop fusion | flops 4718592 | bytes 28311552 | tf_op jit(solution)/shard_map/while/body/eval_jaxpr/add | solution.py:201
  419.3 10.3 %collective-permute-done.1 = bf16[128,768]{1,0:T(8,128)(2,1)S(1)} collective-permute-done((bf16[128,768]{1,0:T(8,128)(2,1)S(1)}, bf16[128,768]{1,0:T(8,128)(2,1)S(1)}, u32[]{:S(2)}, u32[]{:S(2)}) %collective-permute-start.1) | collective-permute-done | bytes 196640 | tf_op jit(solution)/shard_map/while/body/eval_jaxpr/ppermute | solution.py:15
  434.4 14.3 %conditional.6 = (bf16[128,768]{1,0:T(8,128)(2,1)S(1)}, f32[3072,768]{1,0:T(8,128)}, f32[768]{0:T(1024)S(1)}, bf16[128,768]{1,0:T(8,128)(2,1)S(1)}, bf16[128,3072]{1,0:T(8,128)(2,1)S(1)}) conditional(s32[]{:T(128)} %convert_element_type.335, bf16[128,768]{1,0:T(8,128)(2,1)S(1)} %fusion.102, (bf16[128,768]{1,0:T(8,128)(2,1)S(1)}, ...), branch_computations={%region_7.7_spmd, %region_8.13_spmd} | conditional | flops 1828455296 | bytes 46669500 | solution.py:195
  441.9 6.8 fusion.50
  453.9 11.1 %select_add_fusion.4 = f32[3072,768]{1,0:T(8,128)} fusion(f32[3072,768]{1,0:T(8,128)} %get-tuple-element.1150, f32[3072,768]{1,0:T(8,128)} %get-tuple-element.1255, pred[]{:T(512)S(6)} %compare.23), kind=kLoop, calls=%fused_computation.106.clone.1 | loop fusion | flops 4718592 | bytes 28311552 | tf_op jit(solution)/shard_map/while/body/eval_jaxpr/add | solution.py:201
  470.5 14.3 %conditional.6 = (bf16[128,768]{1,0:T(8,128)(2,1)S(1)}, f32[3072,768]{1,0:T(8,128)}, f32[768]{0:T(1024)S(1)}, bf16[128,768]{1,0:T(8,128)(2,1)S(1)}, bf16[128,3072]{1,0:T(8,128)(2,1)S(1)}) conditional(s32[]{:T(128)} %convert_element_type.335, bf16[128,768]{1,0:T(8,128)(2,1)S(1)} %fusion.102, (bf16[128,768]{1,0:T(8,128)(2,1)S(1)}, ...), branch_computations={%region_7.7_spmd, %region_8.13_spmd} | conditional | flops 1828455296 | bytes 46669500 | solution.py:195
  477.9 6.8 fusion.50
  490.0 11.1 %select_add_fusion.4 = f32[3072,768]{1,0:T(8,128)} fusion(f32[3072,768]{1,0:T(8,128)} %get-tuple-element.1150, f32[3072,768]{1,0:T(8,128)} %get-tuple-element.1255, pred[]{:T(512)S(6)} %compare.23), kind=kLoop, calls=%fused_computation.106.clone.1 | loop fusion | flops 4718592 | bytes 28311552 | tf_op jit(solution)/shard_map/while/body/eval_jaxpr/add | solution.py:201
  506.6 14.3 %conditional.6 = (bf16[128,768]{1,0:T(8,128)(2,1)S(1)}, f32[3072,768]{1,0:T(8,128)}, f32[768]{0:T(1024)S(1)}, bf16[128,768]{1,0:T(8,128)(2,1)S(1)}, bf16[128,3072]{1,0:T(8,128)(2,1)S(1)}) conditional(s32[]{:T(128)} %convert_element_type.335, bf16[128,768]{1,0:T(8,128)(2,1)S(1)} %fusion.102, (bf16[128,768]{1,0:T(8,128)(2,1)S(1)}, ...), branch_computations={%region_7.7_spmd, %region_8.13_spmd} | conditional | flops 1828455296 | bytes 46669500 | solution.py:195
  514.0 6.8 fusion.50
  526.1 11.1 %select_add_fusion.4 = f32[3072,768]{1,0:T(8,128)} fusion(f32[3072,768]{1,0:T(8,128)} %get-tuple-element.1150, f32[3072,768]{1,0:T(8,128)} %get-tuple-element.1255, pred[]{:T(512)S(6)} %compare.23), kind=kLoop, calls=%fused_computation.106.clone.1 | loop fusion | flops 4718592 | bytes 28311552 | tf_op jit(solution)/shard_map/while/body/eval_jaxpr/add | solution.py:201
  542.7 14.3 %conditional.6 = (bf16[128,768]{1,0:T(8,128)(2,1)S(1)}, f32[3072,768]{1,0:T(8,128)}, f32[768]{0:T(1024)S(1)}, bf16[128,768]{1,0:T(8,128)(2,1)S(1)}, bf16[128,3072]{1,0:T(8,128)(2,1)S(1)}) conditional(s32[]{:T(128)} %convert_element_type.335, bf16[128,768]{1,0:T(8,128)(2,1)S(1)} %fusion.102, (bf16[128,768]{1,0:T(8,128)(2,1)S(1)}, ...), branch_computations={%region_7.7_spmd, %region_8.13_spmd} | conditional | flops 1828455296 | bytes 46669500 | solution.py:195
  550.1 6.8 fusion.50
  562.2 11.1 %select_add_fusion.4 = f32[3072,768]{1,0:T(8,128)} fusion(f32[3072,768]{1,0:T(8,128)} %get-tuple-element.1150, f32[3072,768]{1,0:T(8,128)} %get-tuple-element.1255, pred[]{:T(512)S(6)} %compare.23), kind=kLoop, calls=%fused_computation.106.clone.1 | loop fusion | flops 4718592 | bytes 28311552 | tf_op jit(solution)/shard_map/while/body/eval_jaxpr/add | solution.py:201
  578.7 14.3 %conditional.6 = (bf16[128,768]{1,0:T(8,128)(2,1)S(1)}, f32[3072,768]{1,0:T(8,128)}, f32[768]{0:T(1024)S(1)}, bf16[128,768]{1,0:T(8,128)(2,1)S(1)}, bf16[128,3072]{1,0:T(8,128)(2,1)S(1)}) conditional(s32[]{:T(128)} %convert_element_type.335, bf16[128,768]{1,0:T(8,128)(2,1)S(1)} %fusion.102, (bf16[128,768]{1,0:T(8,128)(2,1)S(1)}, ...), branch_computations={%region_7.7_spmd, %region_8.13_spmd} | conditional | flops 1828455296 | bytes 46669500 | solution.py:195
  586.2 6.8 fusion.50
  598.3 11.1 %select_add_fusion.4 = f32[3072,768]{1,0:T(8,128)} fusion(f32[3072,768]{1,0:T(8,128)} %get-tuple-element.1150, f32[3072,768]{1,0:T(8,128)} %get-tuple-element.1255, pred[]{:T(512)S(6)} %compare.23), kind=kLoop, calls=%fused_computation.106.clone.1 | loop fusion | flops 4718592 | bytes 28311552 | tf_op jit(solution)/shard_map/while/body/eval_jaxpr/add | solution.py:201
  614.9 14.3 %conditional.6 = (bf16[128,768]{1,0:T(8,128)(2,1)S(1)}, f32[3072,768]{1,0:T(8,128)}, f32[768]{0:T(1024)S(1)}, bf16[128,768]{1,0:T(8,128)(2,1)S(1)}, bf16[128,3072]{1,0:T(8,128)(2,1)S(1)}) conditional(s32[]{:T(128)} %convert_element_type.335, bf16[128,768]{1,0:T(8,128)(2,1)S(1)} %fusion.102, (bf16[128,768]{1,0:T(8,128)(2,1)S(1)}, ...), branch_computations={%region_7.7_spmd, %region_8.13_spmd} | conditional | flops 1828455296 | bytes 46669500 | solution.py:195
  622.3 6.8 fusion.50
  634.4 11.1 %select_add_fusion.4 = f32[3072,768]{1,0:T(8,128)} fusion(f32[3072,768]{1,0:T(8,128)} %get-tuple-element.1150, f32[3072,768]{1,0:T(8,128)} %get-tuple-element.1255, pred[]{:T(512)S(6)} %compare.23), kind=kLoop, calls=%fused_computation.106.clone.1 | loop fusion | flops 4718592 | bytes 28311552 | tf_op jit(solution)/shard_map/while/body/eval_jaxpr/add | solution.py:201
  650.9 14.3 %conditional.6 = (bf16[128,768]{1,0:T(8,128)(2,1)S(1)}, f32[3072,768]{1,0:T(8,128)}, f32[768]{0:T(1024)S(1)}, bf16[128,768]{1,0:T(8,128)(2,1)S(1)}, bf16[128,3072]{1,0:T(8,128)(2,1)S(1)}) conditional(s32[]{:T(128)} %convert_element_type.335, bf16[128,768]{1,0:T(8,128)(2,1)S(1)} %fusion.102, (bf16[128,768]{1,0:T(8,128)(2,1)S(1)}, ...), branch_computations={%region_7.7_spmd, %region_8.13_spmd} | conditional | flops 1828455296 | bytes 46669500 | solution.py:195
  658.4 6.8 fusion.50
  670.5 11.1 %select_add_fusion.4 = f32[3072,768]{1,0:T(8,128)} fusion(f32[3072,768]{1,0:T(8,128)} %get-tuple-element.1150, f32[3072,768]{1,0:T(8,128)} %get-tuple-element.1255, pred[]{:T(512)S(6)} %compare.23), kind=kLoop, calls=%fused_computation.106.clone.1 | loop fusion | flops 4718592 | bytes 28311552 | tf_op jit(solution)/shard_map/while/body/eval_jaxpr/add | solution.py:201
  687.0 14.3 %conditional.6 = (bf16[128,768]{1,0:T(8,128)(2,1)S(1)}, f32[3072,768]{1,0:T(8,128)}, f32[768]{0:T(1024)S(1)}, bf16[128,768]{1,0:T(8,128)(2,1)S(1)}, bf16[128,3072]{1,0:T(8,128)(2,1)S(1)}) conditional(s32[]{:T(128)} %convert_element_type.335, bf16[128,768]{1,0:T(8,128)(2,1)S(1)} %fusion.102, (bf16[128,768]{1,0:T(8,128)(2,1)S(1)}, ...), branch_computations={%region_7.7_spmd, %region_8.13_spmd} | conditional | flops 1828455296 | bytes 46669500 | solution.py:195
  694.5 6.8 fusion.50
  706.6 11.1 %select_add_fusion.4 = f32[3072,768]{1,0:T(8,128)} fusion(f32[3072,768]{1,0:T(8,128)} %get-tuple-element.1150, f32[3072,768]{1,0:T(8,128)} %get-tuple-element.1255, pred[]{:T(512)S(6)} %compare.23), kind=kLoop, calls=%fused_computation.106.clone.1 | loop fusion | flops 4718592 | bytes 28311552 | tf_op jit(solution)/shard_map/while/body/eval_jaxpr/add | solution.py:201
  718.7 9.1 %bitcast_convert_fusion = bf16[768,3072]{1,0:T(8,128)(2,1)} fusion(bf16[8,128,768]{2,1,0:T(8,128)(2,1)} %get-tuple-element.809, bf16[8,128,3072]{2,1,0:T(8,128)(2,1)} %get-tuple-element.810), kind=kOutput, calls=%fused_computation.121 | convolution fusion | flops 4834197504 | bytes 12582912 | tf_op jit(solution)/shard_map/dot_general | solution.py:82
  727.9 6.3 convert_bitcast_fusion
  734.1 17.0 %reduce-scatter.10.cloned.1.call-done = bf16[96,1]{1,0:T(8,128)(2,1)} async-done(((bf16[768,1]{1,0:T(8,128)(2,1)}), bf16[96,1]{1,0:T(8,128)(2,1)}) %reduce-scatter.10.cloned.1.call-update) | async-done | bytes 208
  752.5 53.9 %reduce-scatter.6.cloned.1.call-done = bf16[96,3072]{1,0:T(8,128)(2,1)} async-done(((bf16[768,3072]{1,0:T(8,128)(2,1)}), bf16[96,3072]{1,0:T(8,128)(2,1)}) %reduce-scatter.6.cloned.1.call-update) | async-done | bytes 589840 | tf_op jit(solution)/shard_map/reduce_scatter | solution.py:221
  808.5 53.3 %reduce-scatter.8.cloned.1.call-done = bf16[1,384,768]{2,1,0:T(8,128)(2,1)} async-done(((bf16[1,3072,768]{2,1,0:T(8,128)(2,1)}), bf16[1,384,768]{2,1,0:T(8,128)(2,1)}) %reduce-scatter.8.cloned.1.call-update) | async-done | bytes 589840 | tf_op jit(solution)/shard_map/reduce_scatter | solution.py:229
  (550 shorter events, 378.5 us)
Async XLA Ops:
  7.2 56.9 %all-gather.3.cloned.1.call-start = ((), (), s32[]{:S(2)}) async-start(), calls=%async_computation.3 | async-start | bytes 5308416 | tf_op jit(solution)/shard_map/all_gather | solution.py:96
  7.9 107.7 %all-gather.5.cloned.1.call-start = ((), (), s32[]{:S(2)}) async-start(), calls=%async_computation.4 | async-start | bytes 5308416 | tf_op jit(solution)/shard_map/all_gather | solution.py:97
  8.6 742.5 %reduce-scatter.10.cloned.1.call-start = ((), (), s32[]{:S(2)}) async-start(), calls=%async_computation.7 | async-start | bytes 221184
  134.8 6.1 collective-permute-start
  153.3 8.7 %collective-permute-start = (bf16[128,768]{1,0:T(8,128)(2,1)S(1)}, bf16[128,768]{1,0:T(8,128)(2,1)S(1)}, u32[]{:S(2)}, u32[]{:S(2)}) collective-permute-start(bf16[128,768]{1,0:T(8,128)(2,1)S(1)} %get-tuple-element.1128), channel_id=1, source_target_pairs={{0,8},{8,16},{16,24},{1,9},{9,17},{17,25},{2,10},{10,18},{18,26},{... | collective-permute-start | bytes 589832 | tf_op jit(solution)/shard_map/while/body/eval_jaxpr/ppermute | solution.py:15
  174.4 8.4 collective-permute-start
  195.2 7.6 collective-permute-start
  215.1 8.6 collective-permute-start
  236.1 8.5 collective-permute-start
  257.0 8.4 collective-permute-start
  277.8 8.5 collective-permute-start
  292.6 13.4 %collective-permute-start = (bf16[128,768]{1,0:T(8,128)(2,1)S(1)}, bf16[128,768]{1,0:T(8,128)(2,1)S(1)}, u32[]{:S(2)}, u32[]{:S(2)}) collective-permute-start(bf16[128,768]{1,0:T(8,128)(2,1)S(1)} %get-tuple-element.1128), channel_id=1, source_target_pairs={{0,8},{8,16},{16,24},{1,9},{9,17},{17,25},{2,10},{10,18},{18,26},{... | collective-permute-start | bytes 589832 | tf_op jit(solution)/shard_map/while/body/eval_jaxpr/ppermute | solution.py:15
  312.2 8.4 collective-permute-start
  326.9 13.5 %collective-permute-start = (bf16[128,768]{1,0:T(8,128)(2,1)S(1)}, bf16[128,768]{1,0:T(8,128)(2,1)S(1)}, u32[]{:S(2)}, u32[]{:S(2)}) collective-permute-start(bf16[128,768]{1,0:T(8,128)(2,1)S(1)} %get-tuple-element.1128), channel_id=1, source_target_pairs={{0,8},{8,16},{16,24},{1,9},{9,17},{17,25},{2,10},{10,18},{18,26},{... | collective-permute-start | bytes 589832 | tf_op jit(solution)/shard_map/while/body/eval_jaxpr/ppermute | solution.py:15
  354.5 13.7 %collective-permute-start.1 = (bf16[128,768]{1,0:T(8,128)(2,1)S(1)}, bf16[128,768]{1,0:T(8,128)(2,1)S(1)}, u32[]{:S(2)}, u32[]{:S(2)}) collective-permute-start(bf16[128,768]{1,0:T(8,128)(2,1)S(1)} %get-tuple-element.1149), channel_id=1, source_target_pairs={{8,0},{16,8},{24,16},{9,1},{17,9},{25,17},{10,2},{18,10},{26,18},{... | collective-permute-start | bytes 589832 | tf_op jit(solution)/shard_map/while/body/eval_jaxpr/ppermute | solution.py:15
  377.4 16.4 %collective-permute-start.1 = (bf16[128,768]{1,0:T(8,128)(2,1)S(1)}, bf16[128,768]{1,0:T(8,128)(2,1)S(1)}, u32[]{:S(2)}, u32[]{:S(2)}) collective-permute-start(bf16[128,768]{1,0:T(8,128)(2,1)S(1)} %get-tuple-element.1149), channel_id=1, source_target_pairs={{8,0},{16,8},{24,16},{9,1},{17,9},{25,17},{10,2},{18,10},{26,18},{... | collective-permute-start | bytes 589832 | tf_op jit(solution)/shard_map/while/body/eval_jaxpr/ppermute | solution.py:15
  402.9 26.7 %collective-permute-start.1 = (bf16[128,768]{1,0:T(8,128)(2,1)S(1)}, bf16[128,768]{1,0:T(8,128)(2,1)S(1)}, u32[]{:S(2)}, u32[]{:S(2)}) collective-permute-start(bf16[128,768]{1,0:T(8,128)(2,1)S(1)} %get-tuple-element.1149), channel_id=1, source_target_pairs={{8,0},{16,8},{24,16},{9,1},{17,9},{25,17},{10,2},{18,10},{26,18},{... | collective-permute-start | bytes 589832 | tf_op jit(solution)/shard_map/while/body/eval_jaxpr/ppermute | solution.py:15
  434.6 5.2 slice-start
  434.8 5.0 slice-start.1
  441.8 6.9 copy-start.1
  448.7 17.0 %collective-permute-start.1 = (bf16[128,768]{1,0:T(8,128)(2,1)S(1)}, bf16[128,768]{1,0:T(8,128)(2,1)S(1)}, u32[]{:S(2)}, u32[]{:S(2)}) collective-permute-start(bf16[128,768]{1,0:T(8,128)(2,1)S(1)} %get-tuple-element.1149), channel_id=1, source_target_pairs={{8,0},{16,8},{24,16},{9,1},{17,9},{25,17},{10,2},{18,10},{26,18},{... | collective-permute-start | bytes 589832 | tf_op jit(solution)/shard_map/while/body/eval_jaxpr/ppermute | solution.py:15
  470.6 5.2 slice-start
  470.9 5.0 slice-start.1
  477.9 6.9 copy-start.1
  484.8 17.0 %collective-permute-start.1 = (bf16[128,768]{1,0:T(8,128)(2,1)S(1)}, bf16[128,768]{1,0:T(8,128)(2,1)S(1)}, u32[]{:S(2)}, u32[]{:S(2)}) collective-permute-start(bf16[128,768]{1,0:T(8,128)(2,1)S(1)} %get-tuple-element.1149), channel_id=1, source_target_pairs={{8,0},{16,8},{24,16},{9,1},{17,9},{25,17},{10,2},{18,10},{26,18},{... | collective-permute-start | bytes 589832 | tf_op jit(solution)/shard_map/while/body/eval_jaxpr/ppermute | solution.py:15
  506.7 5.2 slice-start
  507.0 5.0 slice-start.1
  514.0 6.9 copy-start.1
  520.9 17.0 %collective-permute-start.1 = (bf16[128,768]{1,0:T(8,128)(2,1)S(1)}, bf16[128,768]{1,0:T(8,128)(2,1)S(1)}, u32[]{:S(2)}, u32[]{:S(2)}) collective-permute-start(bf16[128,768]{1,0:T(8,128)(2,1)S(1)} %get-tuple-element.1149), channel_id=1, source_target_pairs={{8,0},{16,8},{24,16},{9,1},{17,9},{25,17},{10,2},{18,10},{26,18},{... | collective-permute-start | bytes 589832 | tf_op jit(solution)/shard_map/while/body/eval_jaxpr/ppermute | solution.py:15
  542.8 5.2 slice-start
  550.1 6.9 copy-start.1
  557.0 17.0 %collective-permute-start.1 = (bf16[128,768]{1,0:T(8,128)(2,1)S(1)}, bf16[128,768]{1,0:T(8,128)(2,1)S(1)}, u32[]{:S(2)}, u32[]{:S(2)}) collective-permute-start(bf16[128,768]{1,0:T(8,128)(2,1)S(1)} %get-tuple-element.1149), channel_id=1, source_target_pairs={{8,0},{16,8},{24,16},{9,1},{17,9},{25,17},{10,2},{18,10},{26,18},{... | collective-permute-start | bytes 589832 | tf_op jit(solution)/shard_map/while/body/eval_jaxpr/ppermute | solution.py:15
  578.9 5.2 slice-start
  579.1 5.0 slice-start.1
  586.2 6.9 copy-start.1
  593.0 17.0 %collective-permute-start.1 = (bf16[128,768]{1,0:T(8,128)(2,1)S(1)}, bf16[128,768]{1,0:T(8,128)(2,1)S(1)}, u32[]{:S(2)}, u32[]{:S(2)}) collective-permute-start(bf16[128,768]{1,0:T(8,128)(2,1)S(1)} %get-tuple-element.1149), channel_id=1, source_target_pairs={{8,0},{16,8},{24,16},{9,1},{17,9},{25,17},{10,2},{18,10},{26,18},{... | collective-permute-start | bytes 589832 | tf_op jit(solution)/shard_map/while/body/eval_jaxpr/ppermute | solution.py:15
  615.0 5.2 slice-start
  622.3 6.9 copy-start.1
  629.2 17.0 %collective-permute-start.1 = (bf16[128,768]{1,0:T(8,128)(2,1)S(1)}, bf16[128,768]{1,0:T(8,128)(2,1)S(1)}, u32[]{:S(2)}, u32[]{:S(2)}) collective-permute-start(bf16[128,768]{1,0:T(8,128)(2,1)S(1)} %get-tuple-element.1149), channel_id=1, source_target_pairs={{8,0},{16,8},{24,16},{9,1},{17,9},{25,17},{10,2},{18,10},{26,18},{... | collective-permute-start | bytes 589832 | tf_op jit(solution)/shard_map/while/body/eval_jaxpr/ppermute | solution.py:15
  651.1 5.2 slice-start
  651.3 5.0 slice-start.1
  658.4 6.9 copy-start.1
  665.2 17.0 %collective-permute-start.1 = (bf16[128,768]{1,0:T(8,128)(2,1)S(1)}, bf16[128,768]{1,0:T(8,128)(2,1)S(1)}, u32[]{:S(2)}, u32[]{:S(2)}) collective-permute-start(bf16[128,768]{1,0:T(8,128)(2,1)S(1)} %get-tuple-element.1149), channel_id=1, source_target_pairs={{8,0},{16,8},{24,16},{9,1},{17,9},{25,17},{10,2},{18,10},{26,18},{... | collective-permute-start | bytes 589832 | tf_op jit(solution)/shard_map/while/body/eval_jaxpr/ppermute | solution.py:15
  687.2 5.2 slice-start
  694.5 6.9 copy-start.1
  701.3 16.4 %collective-permute-start.1 = (bf16[128,768]{1,0:T(8,128)(2,1)S(1)}, bf16[128,768]{1,0:T(8,128)(2,1)S(1)}, u32[]{:S(2)}, u32[]{:S(2)}) collective-permute-start(bf16[128,768]{1,0:T(8,128)(2,1)S(1)} %get-tuple-element.1149), channel_id=1, source_target_pairs={{8,0},{16,8},{24,16},{9,1},{17,9},{25,17},{10,2},{18,10},{26,18},{... | collective-permute-start | bytes 589832 | tf_op jit(solution)/shard_map/while/body/eval_jaxpr/ppermute | solution.py:15
  718.6 87.7 %reduce-scatter.6.cloned.1.call-start = ((), (), s32[]{:S(2)}) async-start(), calls=%async_computation.5 | async-start | bytes 5308416 | tf_op jit(solution)/shard_map/reduce_scatter | solution.py:221
  727.8 134.0 %reduce-scatter.8.cloned.1.call-start = ((), (), s32[]{:S(2)}) async-start(), calls=%async_computation.6 | async-start | bytes 5308416 | tf_op jit(solution)/shard_map/reduce_scatter | solution.py:229
  (22 other events, 68.4 us)
Sparse Core Ops, SparseCore 0:
  9.6 54.3 all-gather.2
  65.7 49.8 all-gather.4
  718.7 32.3 reduce-scatter.9
  753.3 53.0 reduce-scatter.5
  808.5 53.3 reduce-scatter.7
where the time goes:
time: 874 us; the launch traced here: 871 us
  waiting for transfers between devices  227 us (26%)
  other arithmetic  207 us (24%)
  matrix products  175 us (20%)
  local copies, waits for them, and re-layouts  113 us (13%)
  starting transfers between devices  69.8 us (8%)
  loops' own time  46 us (5%)
  blocking collectives  18.8 us (2%)
  between operations  14.5 us (2%)
    add x11, other arithmetic, backward_tick(): acc_down = acc_down + term_down  120 us
    ppermute x22, starting transfers between devices, passed_along(): return lax.ppermute(block, axis, route)  69.6 us
    dot_general x9, matrix products, contract_rows(): lax.dot_general(left, right, (((0,), (0,)), ((), ())), preferred_element_...  63.8 us
    dynamic_update_slice x44, other arithmetic, store_row(): return lax.dynamic_update_index_in_dim(stash, row, slot, 0)  57.6 us
    reduce_scatter x1, waiting for transfers between devices, per_device(): lax.psum_scatter(contract_rows(flat_normed, flat_grad).astype(jnp.bfloat1...  53.9 us
    reduce_scatter x1, waiting for transfers between devices, per_device(): lax.psum_scatter(acc_down[None].astype(jnp.bfloat16), 'fsdp', scatter_dim...  53.3 us
    all_gather x1, waiting for transfers between devices, per_device(): lax.all_gather(w_down, 'fsdp', axis=1, tiled=True)  51.6 us
    dynamic_slice x44, local copies, waits for them, and re-layouts, store_row(): row = jnp.where(is_valid, value, stash[slot])  40.5 us
  transfers between devices with their start and end apart: 27, of which 17 were waited for; matrix products, arithmetic and copies ran while one was open for 26% of the time, Pallas kernels for 0%

commit v1 on v0

v1 whole, which is shorter than its diff:
```python
import jax
import jax.numpy as jnp
from jax import lax
from jax.sharding import PartitionSpec as P

BLOCK = 128


EPSILON = 1e-05


def passed_along(block, axis, distance):
    devices = range(lax.axis_size(axis))
    route = [(i - distance, i) for i in devices if i - distance in devices]
    return lax.ppermute(block, axis, route)


def micro_masks(blocks, ratio, feature_count, hidden_count):
    width_int = blocks * BLOCK
    hidden_int = width_int * (6 + ratio) // 2
    embed_mask = (lax.iota(jnp.int32, feature_count) < width_int).astype(jnp.float32)
    hidden_mask = (lax.iota(jnp.int32, hidden_count) < hidden_int).astype(jnp.float32)
    return (embed_mask, hidden_mask, width_int.astype(jnp.float32))


def layer_norm(inputs, embed_mask, width_float):
    values = inputs.astype(jnp.float32) * embed_mask
    center_value = jnp.sum(values, axis=-1, keepdims=True) / width_float
    centered = (values - center_value) * embed_mask
    variance = jnp.sum(centered * centered, axis=-1, keepdims=True) / width_float
    inv_std = lax.rsqrt(variance + EPSILON)
    return (centered * inv_std, inv_std)


def run_ticks(total, tick, carry):
    for number in range(total):
        carry = tick(number, carry)
    return carry


def gelu_and_slope(hidden):
    square = hidden * hidden
    scale = 0.7978845608028654
    tanh = jnp.tanh(scale * hidden * (1.0 + 0.044715 * square))
    half = 0.5 * (1.0 + tanh)
    slope = half + (0.5 * scale) * hidden * (1.0 - tanh * tanh) * (1.0 + 0.134145 * square)
    return (hidden * half, slope)


def contract_rows(left, right):
    return lax.dot_general(
        left, right, (((0,), (0,)), ((), ())), preferred_element_type=jnp.float32
    )


def contract_last(left, right):
    return lax.dot_general(
        left, right, (((1,), (1,)), ((), ())), preferred_element_type=jnp.float32
    )


def store_row(stash, value, slot):
    return lax.dynamic_update_index_in_dim(stash, value, slot, 0)


HOP_TICKS = 2
EXTRA_ROWS = 16


def per_device(patches, cotangent, embed_blocks, ratio_index, depth, w_up, w_down, ln_gain):
    section_count = lax.axis_size("section")
    section_index = lax.axis_index("section")
    shard_count = lax.axis_size("fsdp")
    micro_count, row_count, feature_count = patches.shape
    hidden_count = w_up.shape[2]
    down_rows = w_down.shape[1]
    gain_count = ln_gain.shape[1]
    tick_total = micro_count + HOP_TICKS * (section_count - 1)
    bf16 = jnp.bfloat16

    gain_rows = jnp.pad(ln_gain, ((0, EXTRA_ROWS - 1), (0, feature_count - gain_count)))
    packed_down = jnp.concatenate([w_down[0], gain_rows], axis=0)
    weight_up = lax.all_gather(w_up[0], "fsdp", axis=0, tiled=True)
    gathered_down = lax.all_gather(packed_down, "fsdp", axis=0, tiled=True)
    gathered_down = gathered_down.reshape(shard_count, down_rows + EXTRA_ROWS, feature_count)
    weight_down = gathered_down[:, :down_rows].reshape(hidden_count, feature_count)
    gain = gathered_down[:, down_rows, :gain_count].reshape(feature_count).astype(jnp.float32)

    def masks_of(micro_index):
        is_valid = jnp.logical_and(micro_index >= 0, micro_index < micro_count)
        safe_index = jnp.clip(micro_index, 0, micro_count - 1)
        slot = jnp.where(is_valid, micro_index, micro_count)
        embed_mask, hidden_mask, width_float = micro_masks(
            embed_blocks[safe_index], ratio_index[safe_index], feature_count, hidden_count
        )
        active = (section_index < depth[safe_index]).astype(jnp.float32)
        return (safe_index, slot, is_valid, embed_mask, hidden_mask, active, width_float)

    def forward_tick(tick, carry):
        previous, incoming, stash_in, stash_act, stash_slope = carry
        sent = passed_along(previous, "section", 1)
        safe, slot, is_valid, embed_mask, hidden_mask, active, width = masks_of(
            tick - HOP_TICKS * section_index
        )
        first_in = (patches[safe].astype(jnp.float32) * embed_mask).astype(bf16)
        inputs = jnp.where(section_index == 0, first_in, incoming)
        standard, inv_std = layer_norm(inputs, embed_mask, width)
        normed = (standard * gain).astype(bf16)
        hidden = jnp.dot(normed, weight_up, preferred_element_type=jnp.float32)
        value, slope = gelu_and_slope(hidden)
        act = (value * hidden_mask).astype(bf16)
        slope = (slope * hidden_mask).astype(bf16)
        branch = jnp.dot(act, weight_down, preferred_element_type=jnp.float32)
        output = (inputs.astype(jnp.float32) + active * embed_mask * branch).astype(bf16)
        return (
            output,
            sent,
            store_row(stash_in, inputs, slot),
            store_row(stash_act, act, slot),
            store_row(stash_slope, slope, slot),
        )

    def empty(width):
        return jnp.zeros((micro_count + 1, row_count, width), bf16)

    nothing = jnp.zeros((row_count, feature_count), bf16)
    carry = (nothing, nothing, empty(feature_count), empty(hidden_count), empty(hidden_count))
    carry = run_ticks(tick_total, forward_tick, carry)
    unused_out, unused_sent, stash_in, stash_act, stash_slope = carry

    def backward_tick(tick, carry):
        previous, incoming, acc_gain, stash_branch, stash_hidden, stash_normed = carry
        sent = passed_along(previous, "section", -1)
        safe, slot, is_valid, embed_mask, hidden_mask, active, width = masks_of(
            tick - HOP_TICKS * (section_count - 1 - section_index)
        )
        last_in = (cotangent[safe].astype(jnp.float32) * embed_mask).astype(bf16)
        grad_out = jnp.where(section_index == section_count - 1, last_in, incoming)
        grad_float = grad_out.astype(jnp.float32)
        live = jnp.where(is_valid, active, 0.0)
        grad_branch = (live * embed_mask * grad_float).astype(bf16)
        grad_act = contract_last(grad_branch, weight_down)
        grad_hidden = (grad_act * stash_slope[slot].astype(jnp.float32)).astype(bf16)
        grad_normed = contract_last(grad_hidden, weight_up)
        standard, inv_std = layer_norm(stash_in[slot], embed_mask, width)
        normed = (standard * gain).astype(bf16)
        grad_standard = grad_normed * gain * embed_mask
        acc_gain = acc_gain + jnp.sum(grad_normed * standard, axis=0)
        first_mean = jnp.sum(grad_standard, axis=-1, keepdims=True) / width
        second_mean = jnp.sum(grad_standard * standard, axis=-1, keepdims=True) / width
        grad_norm_in = inv_std * (grad_standard - first_mean * embed_mask - standard * second_mean)
        grad_in = (grad_float + grad_norm_in).astype(bf16)
        return (
            grad_in,
            sent,
            acc_gain,
            store_row(stash_branch, grad_branch, slot),
            store_row(stash_hidden, grad_hidden, slot),
            store_row(stash_normed, normed, slot),
        )

    carry = (
        nothing,
        nothing,
        jnp.zeros((feature_count,), jnp.float32),
        empty(feature_count),
        empty(hidden_count),
        empty(feature_count),
    )
    carry = run_ticks(tick_total, backward_tick, carry)
    unused_out, unused_sent, acc_gain, stash_branch, stash_hidden, stash_normed = carry

    def flat(stash):
        return stash.reshape(-1, stash.shape[-1])

    part_down = contract_rows(flat(stash_act), flat(stash_branch)).astype(bf16)
    part_gain = acc_gain.astype(bf16).reshape(shard_count, 1, gain_count)
    part_gain = jnp.pad(
        part_gain, ((0, 0), (0, EXTRA_ROWS - 1), (0, feature_count - gain_count))
    )
    packed = jnp.concatenate(
        [part_down.reshape(shard_count, down_rows, feature_count), part_gain], axis=1
    ).reshape(-1, feature_count)
    own_down = lax.psum_scatter(packed, "fsdp", scatter_dimension=0, tiled=True)
    part_up = contract_rows(flat(stash_normed), flat(stash_hidden)).astype(bf16)
    own_up = lax.psum_scatter(part_up, "fsdp", scatter_dimension=0, tiled=True)
    grad_up = own_up.astype(jnp.float32)[None]
    grad_down = own_down[:down_rows].astype(jnp.float32)[None]
    grad_gain = own_down[down_rows, :gain_count].astype(jnp.float32)[None]
    return (grad_up, grad_down, grad_gain)


def solution(mesh):
    return jax.shard_map(
        per_device,
        mesh=mesh,
        in_specs=(
            P(None, "fsdp", None),
            P(None, "fsdp", None),
            P(),
            P(),
            P(),
            P("section", "fsdp", None),
            P("section", "fsdp", None),
            P("section", "fsdp"),
        ),
        out_specs=(P("section", "fsdp", None), P("section", "fsdp", None), P("section", "fsdp")),
        check_vma=False,
    )
```

time: 874 us -> 542 us (0.62)
  other arithmetic: 207 us -> 75.4 us
  local copies, waits for them, and re-layouts: 113 us -> 21.9 us
  matrix products: 175 us -> 116 us
  loops' own time: 46 us -> 0 us
  between operations: 14.5 us -> 59.9 us
  waiting for transfers between devices: 227 us -> 189 us
  blocking collectives: 18.8 us -> 0 us
    add x22 -> x0, other arithmetic: 120 us -> none  [the longest x11 120 us: backward_tick(): acc_down = acc_down + term_down]
    all_gather x2, waiting for transfers between devices: 85.3 us -> 3.03 us  [the longest x1 3.03 us: per_device(): weight_up = lax.all_gather(w_up[0], 'fsdp', axis=0, tiled=True)]
    ppermute x22 -> x26, waiting for transfers between devices: 16.3 us -> 97.3 us  [passed_along(): return lax.ppermute(block, axis, route)]
    dynamic_slice x66 -> x0, local copies, waits for them, and re-layouts: 53.7 us -> none  [the longest x44 40.5 us: store_row(): row = jnp.where(is_valid, value, stash[slot])]
    dot_general x9 -> x2, matrix products: 63.8 us -> 17.2 us  [contract_rows(): lax.dot_general(left, right, (((0,), (0,)), ((), ())), preferred_element_...]
    another operation x24 -> x0, loops' own time: 46 us -> none  [the longest x1 22.4 us: per_device(): lax.fori_loop(0, tick_total, backward_tick, back_carry)]
    dynamic_update_slice x44 -> x36, other arithmetic: 57.6 us -> 18.5 us  [store_row(): return lax.dynamic_update_index_in_dim(stash, value, slot, 0)]
    squeeze x1 -> x0, blocking collectives: 18.8 us -> none  [per_device(): gain_vector = gathered_gain[0]]
  transfers between devices with their start and end apart: 27 -> 30, of which waited for: 17 -> 20; matrix products, arithmetic and copies ran while one was open for 26% -> 23% of each run, Pallas kernels for 0% -> 0%
where the time goes in v1:
time: 542 us; the launch traced here: 531 us
  waiting for transfers between devices  189 us (35%)
  matrix products  116 us (21%)
  other arithmetic  75.4 us (14%)
  starting transfers between devices  69.7 us (13%)
  between operations  59.9 us (11%)
  local copies, waits for them, and re-layouts  21.9 us (4%)
    ppermute x26, waiting for transfers between devices, passed_along(): return lax.ppermute(block, axis, route)  97.3 us
    ppermute x26, starting transfers between devices, passed_along(): return lax.ppermute(block, axis, route)  69.5 us
    dot_general x28, matrix products, contract_last(): lax.dot_general(left, right, (((1,), (1,)), ((), ())), preferred_element_...  57.3 us
    reduce_scatter x1, waiting for transfers between devices, per_device(): own_down = lax.psum_scatter(packed, 'fsdp', scatter_dimension=0, tiled=True)  55.2 us
    reduce_scatter x1, waiting for transfers between devices, per_device(): own_up = lax.psum_scatter(part_up, 'fsdp', scatter_dimension=0, tiled=True)  33.2 us
    dot_general x14, matrix products, forward_tick(): hidden = jnp.dot(normed, weight_up, preferred_element_type=jnp.float32)  27.5 us
    dynamic_update_slice x36, other arithmetic, store_row(): return lax.dynamic_update_index_in_dim(stash, value, slot, 0)  18.5 us
    dot_general x2, matrix products, contract_rows(): lax.dot_general(left, right, (((0,), (0,)), ((), ())), preferred_element_...  17.2 us
  transfers between devices with their start and end apart: 30, of which 20 were waited for; matrix products, arithmetic and copies ran while one was open for 23% of the time, Pallas kernels for 0%

profile of v1, /device:TPU:0, one launch (start us, length us, event | category | flops | bytes accessed | tf_op | source)
XLA Modules:
  0.0 531.3 jit_solution(3041586789958740881)
XLA Ops:
  11.3 6.2 %collective-permute-start = (bf16[128,768]{1,0:T(8,128)(2,1)}, bf16[128,768]{1,0:T(8,128)(2,1)}, u32[]{:S(2)}, u32[]{:S(2)}) collective-permute-start(bf16[128,768]{1,0:T(8,128)(2,1)} %broadcast_in_dim.237), channel_id=1, source_target_pairs={{0,8},{8,16},{16,24},{1,9},{9,17},{17,25},{2,10},{10,18},{18,26},{... | collective-permute-start | bytes 589832 | tf_op jit(solution)/shard_map/ppermute | solution.py:15
  107.6 4.8 slice.17
  114.6 3.0 all-gather.6.cloned.1.call-done
  120.5 2.5 bitcast_dynamic-update-slice_fusion.13
  123.8 2.5 bitcast_dynamic-update-slice_fusion.41
  127.6 3.4 collective-permute-start.1
  134.1 3.6 collective-permute-start.2
  138.1 3.6 collective-permute-done.2
  145.3 4.4 collective-permute-start.3
  152.8 4.3 collective-permute-start.4
  157.5 2.7 collective-permute-done.4
  163.8 4.8 collective-permute-start.5
  171.7 3.0 collective-permute-start.6
  175.2 2.7 collective-permute-done.6
  181.5 4.4 collective-permute-start.7
  189.0 3.0 collective-permute-start.8
  192.4 2.5 collective-permute-done.8
  198.5 4.4 collective-permute-start.9
  206.1 2.8 collective-permute-start.10
  209.3 2.7 collective-permute-done.10
  215.5 4.6 collective-permute-start.11
  223.3 2.8 collective-permute-start.12
  226.6 2.7 collective-permute-done.12
  234.0 4.2 broadcast.1352
  238.9 2.5 bitcast_dynamic-update-slice_fusion.27
  241.5 2.5 bitcast_dynamic-update-slice_fusion.26
  249.8 4.6 collective-permute-done.15
  260.1 7.1 %collective-permute-done.17 = bf16[128,768]{1,0:T(8,128)(2,1)S(1)} collective-permute-done((bf16[128,768]{1,0:T(8,128)(2,1)S(1)}, bf16[128,768]{1,0:T(8,128)(2,1)S(1)}, u32[]{:S(2)}, u32[]{:S(2)}) %collective-permute-start.17) | collective-permute-done | bytes 196640 | tf_op jit(solution)/shard_map/ppermute | solution.py:15
  272.6 7.1 %collective-permute-done.19 = bf16[128,768]{1,0:T(8,128)(2,1)S(1)} collective-permute-done((bf16[128,768]{1,0:T(8,128)(2,1)S(1)}, bf16[128,768]{1,0:T(8,128)(2,1)S(1)}, u32[]{:S(2)}, u32[]{:S(2)}) %collective-permute-start.19) | collective-permute-done | bytes 196640 | tf_op jit(solution)/shard_map/ppermute | solution.py:15
  284.9 7.1 %collective-permute-done.21 = bf16[128,768]{1,0:T(8,128)(2,1)S(1)} collective-permute-done((bf16[128,768]{1,0:T(8,128)(2,1)S(1)}, bf16[128,768]{1,0:T(8,128)(2,1)S(1)}, u32[]{:S(2)}, u32[]{:S(2)}) %collective-permute-start.21) | collective-permute-done | bytes 196640 | tf_op jit(solution)/shard_map/ppermute | solution.py:15
  297.4 7.7 %collective-permute-done.23 = bf16[128,768]{1,0:T(8,128)(2,1)S(1)} collective-permute-done((bf16[128,768]{1,0:T(8,128)(2,1)S(1)}, bf16[128,768]{1,0:T(8,128)(2,1)S(1)}, u32[]{:S(2)}, u32[]{:S(2)}) %collective-permute-start.23) | collective-permute-done | bytes 196640 | tf_op jit(solution)/shard_map/ppermute | solution.py:15
  310.3 7.1 %collective-permute-done.14 = bf16[128,768]{1,0:T(8,128)(2,1)S(1)} collective-permute-done((bf16[128,768]{1,0:T(8,128)(2,1)S(1)}, bf16[128,768]{1,0:T(8,128)(2,1)S(1)}, u32[]{:S(2)}, u32[]{:S(2)}) %collective-permute-start.14) | collective-permute-done | bytes 196640 | tf_op jit(solution)/shard_map/ppermute | solution.py:15
  326.5 8.8 %collective-permute-done.16 = bf16[128,768]{1,0:T(8,128)(2,1)S(1)} collective-permute-done((bf16[128,768]{1,0:T(8,128)(2,1)S(1)}, bf16[128,768]{1,0:T(8,128)(2,1)S(1)}, u32[]{:S(2)}, u32[]{:S(2)}) %collective-permute-start.16) | collective-permute-done | bytes 196640 | tf_op jit(solution)/shard_map/ppermute | solution.py:15
  342.6 9.3 %collective-permute-done.18 = bf16[128,768]{1,0:T(8,128)(2,1)S(1)} collective-permute-done((bf16[128,768]{1,0:T(8,128)(2,1)S(1)}, bf16[128,768]{1,0:T(8,128)(2,1)S(1)}, u32[]{:S(2)}, u32[]{:S(2)}) %collective-permute-start.18) | collective-permute-done | bytes 196640 | tf_op jit(solution)/shard_map/ppermute | solution.py:15
  358.8 8.0 %collective-permute-done.20 = bf16[128,768]{1,0:T(8,128)(2,1)S(1)} collective-permute-done((bf16[128,768]{1,0:T(8,128)(2,1)S(1)}, bf16[128,768]{1,0:T(8,128)(2,1)S(1)}, u32[]{:S(2)}, u32[]{:S(2)}) %collective-permute-start.20) | collective-permute-done | bytes 196640 | tf_op jit(solution)/shard_map/ppermute | solution.py:15
  373.7 6.9 %collective-permute-done.22 = bf16[128,768]{1,0:T(8,128)(2,1)S(1)} collective-permute-done((bf16[128,768]{1,0:T(8,128)(2,1)S(1)}, bf16[128,768]{1,0:T(8,128)(2,1)S(1)}, u32[]{:S(2)}, u32[]{:S(2)}) %collective-permute-start.22) | collective-permute-done | bytes 196640 | tf_op jit(solution)/shard_map/ppermute | solution.py:15
  387.8 6.6 %collective-permute-done.24 = bf16[128,768]{1,0:T(8,128)(2,1)S(1)} collective-permute-done((bf16[128,768]{1,0:T(8,128)(2,1)S(1)}, bf16[128,768]{1,0:T(8,128)(2,1)S(1)}, u32[]{:S(2)}, u32[]{:S(2)}) %collective-permute-start.24) | collective-permute-done | bytes 196640 | tf_op jit(solution)/shard_map/ppermute | solution.py:15
  394.3 2.5 bitcast_dynamic-update-slice_fusion.15
  397.8 2.5 bitcast_dynamic-update-slice_fusion.14
  401.2 8.0 %bitcast_convert_fusion.1 = bf16[768,3072]{1,0:T(8,128)(2,1)} fusion(bf16[9,128,768]{2,1,0:T(8,128)(2,1)S(1)} %get-tuple-element.135, bf16[9,128,3072]{2,1,0:T(8,128)(2,1)S(1)} %get-tuple-element.251), kind=kOutput, calls=%fused_computation.3 | convolution fusion | flops 5438177280 | bytes 13565952 | tf_op jit(solution)/shard_map/dot_general | solution.py:51
  410.3 4.1 fusion.106
  414.4 4.1 fusion.103
  418.7 9.2 %bitcast_convert_fusion = bf16[3072,768]{1,0:T(8,128)(2,1)S(1)} fusion(bf16[9,128,3072]{2,1,0:T(8,128)(2,1)} %copy-done.2, bf16[9,128,768]{2,1,0:T(8,128)(2,1)} %get-tuple-element.134), kind=kOutput, calls=%fused_computation.2 | convolution fusion | flops 5438177280 | bytes 13565952 | tf_op jit(solution)/shard_map/dot_general | solution.py:51
  427.9 2.5 fusion.1
  430.4 33.2 %reduce-scatter.3.cloned.1.call-done = bf16[96,3072]{1,0:T(8,128)(2,1)} async-done(((bf16[768,3072]{1,0:T(8,128)(2,1)}), bf16[96,3072]{1,0:T(8,128)(2,1)}) %reduce-scatter.3.cloned.1.call-update) | async-done | bytes 589840 | tf_op jit(solution)/shard_map/reduce_scatter | solution.py:186
  463.6 2.2 bitcast_convert_fusion.2
  465.8 55.2 %reduce-scatter.5.cloned.1.call-done = bf16[400,768]{1,0:T(8,128)(2,1)} async-done(((bf16[3200,768]{1,0:T(8,128)(2,1)}), bf16[400,768]{1,0:T(8,128)(2,1)}) %reduce-scatter.5.cloned.1.call-update) | async-done | bytes 614416 | tf_op jit(solution)/shard_map/reduce_scatter | solution.py:184
  522.2 2.2 fusion.110
  (508 shorter events, 174.6 us)
Async XLA Ops:
  7.2 10.6 %copy-start.8 = (s32[8]{0:T(128)S(1)}, s32[8]{0:T(128)}, u32[]{:S(2)}) copy-start(s32[8]{0:T(128)} %param.10) | copy-start | bytes 100
  7.2 100.5 %all-gather.4.cloned.1.call-start = ((), (), s32[]{:S(2)}) async-start(), calls=%async_computation.2 | async-start | bytes 5529600 | tf_op jit(solution)/shard_map/all_gather | solution.py:84
  7.2 22.6 %copy-start.9 = (s32[8]{0:T(128)S(1)}, s32[8]{0:T(128)}, u32[]{:S(2)}) copy-start(s32[8]{0:T(128)} %param.12) | copy-start | bytes 100
  7.2 24.0 %copy-start.16 = (s32[8]{0:T(128)S(1)}, s32[8]{0:T(128)}, u32[]{:S(2)}) copy-start(s32[8]{0:T(128)} %param.11) | copy-start | bytes 100
  9.2 108.4 %all-gather.6.cloned.1.call-start = ((), (), s32[]{:S(2)}) async-start(), calls=%async_computation.5 | async-start | bytes 5308416 | tf_op jit(solution)/shard_map/all_gather | solution.py:83
  10.0 95.9 %collective-permute-start.13 = (bf16[128,768]{1,0:T(8,128)(2,1)}, bf16[128,768]{1,0:T(8,128)(2,1)}, u32[]{:S(2)}, u32[]{:S(2)}) collective-permute-start(bf16[128,768]{1,0:T(8,128)(2,1)} %broadcast_in_dim.237), channel_id=1, source_target_pairs={{8,0},{16,8},{24,16},{9,1},{17,9},{25,17},{10,2},{18,10},{26,18},{... | collective-permute-start | bytes 589832 | tf_op jit(solution)/shard_map/ppermute | solution.py:15
  11.3 92.7 %collective-permute-start = (bf16[128,768]{1,0:T(8,128)(2,1)}, bf16[128,768]{1,0:T(8,128)(2,1)}, u32[]{:S(2)}, u32[]{:S(2)}) collective-permute-start(bf16[128,768]{1,0:T(8,128)(2,1)} %broadcast_in_dim.237), channel_id=1, source_target_pairs={{0,8},{8,16},{16,24},{1,9},{9,17},{17,25},{2,10},{10,18},{18,26},{... | collective-permute-start | bytes 589832 | tf_op jit(solution)/shard_map/ppermute | solution.py:15
  17.5 446.1 %reduce-scatter.3.cloned.1.call-start = ((), (), s32[]{:S(2)}) async-start(), calls=%async_computation.3 | async-start | bytes 5308416 | tf_op jit(solution)/shard_map/reduce_scatter | solution.py:186
  72.8 32.3 %copy-start.35 = (f32[768]{0:T(1024)}, f32[768]{0:T(1024)S(1)}, u32[]{:S(2)}) copy-start(f32[768]{0:T(1024)S(1)} %fusion.721) | copy-start | bytes 9220
  72.8 29.9 %copy-start.37 = (f32[768]{0:T(1024)}, f32[768]{0:T(1024)S(1)}, u32[]{:S(2)}) copy-start(f32[768]{0:T(1024)S(1)} %fusion.723) | copy-start | bytes 9220
  79.3 26.6 %copy-start.47 = (f32[768]{0:T(1024)}, f32[768]{0:T(1024)S(1)}, u32[]{:S(2)}) copy-start(f32[768]{0:T(1024)S(1)} %fusion.696) | copy-start | bytes 9220
  79.3 23.3 %copy-start.49 = (f32[768]{0:T(1024)}, f32[768]{0:T(1024)S(1)}, u32[]{:S(2)}) copy-start(f32[768]{0:T(1024)S(1)} %fusion.698) | copy-start | bytes 9220
  89.4 13.3 %copy-start.14 = (f32[768]{0:T(1024)}, f32[768]{0:T(1024)S(1)}, u32[]{:S(2)}) copy-start(f32[768]{0:T(1024)S(1)} %get-tuple-element.272) | copy-start | bytes 9220
  127.6 10.1 %collective-permute-start.1 = (bf16[128,768]{1,0:T(8,128)(2,1)S(1)}, bf16[128,768]{1,0:T(8,128)(2,1)S(1)}, u32[]{:S(2)}, u32[]{:S(2)}) collective-permute-start(bf16[128,768]{1,0:T(8,128)(2,1)S(1)} %fusion.91), channel_id=1, source_target_pairs={{0,8},{8,16},{16,24},{1,9},{9,17},{17,25},{2,10},{10,18},{18,26},{... | collective-permute-start | bytes 589832 | tf_op jit(solution)/shard_map/ppermute | solution.py:15
  134.1 7.6 %collective-permute-start.2 = (bf16[128,768]{1,0:T(8,128)(2,1)S(1)}, bf16[128,768]{1,0:T(8,128)(2,1)S(1)}, u32[]{:S(2)}, u32[]{:S(2)}) collective-permute-start(bf16[128,768]{1,0:T(8,128)(2,1)S(1)} %fusion.92), channel_id=1, source_target_pairs={{0,8},{8,16},{16,24},{1,9},{9,17},{17,25},{2,10},{10,18},{18,26},{... | collective-permute-start | bytes 589832 | tf_op jit(solution)/shard_map/ppermute | solution.py:15
  145.3 11.8 %collective-permute-start.3 = (bf16[128,768]{1,0:T(8,128)(2,1)S(1)}, bf16[128,768]{1,0:T(8,128)(2,1)S(1)}, u32[]{:S(2)}, u32[]{:S(2)}) collective-permute-start(bf16[128,768]{1,0:T(8,128)(2,1)S(1)} %fusion.93), channel_id=1, source_target_pairs={{0,8},{8,16},{16,24},{1,9},{9,17},{17,25},{2,10},{10,18},{18,26},{... | collective-permute-start | bytes 589832 | tf_op jit(solution)/shard_map/ppermute | solution.py:15
  152.8 7.4 %collective-permute-start.4 = (bf16[128,768]{1,0:T(8,128)(2,1)S(1)}, bf16[128,768]{1,0:T(8,128)(2,1)S(1)}, u32[]{:S(2)}, u32[]{:S(2)}) collective-permute-start(bf16[128,768]{1,0:T(8,128)(2,1)S(1)} %fusion.94), channel_id=1, source_target_pairs={{0,8},{8,16},{16,24},{1,9},{9,17},{17,25},{2,10},{10,18},{18,26},{... | collective-permute-start | bytes 589832 | tf_op jit(solution)/shard_map/ppermute | solution.py:15
  163.8 11.0 %collective-permute-start.5 = (bf16[128,768]{1,0:T(8,128)(2,1)S(1)}, bf16[128,768]{1,0:T(8,128)(2,1)S(1)}, u32[]{:S(2)}, u32[]{:S(2)}) collective-permute-start(bf16[128,768]{1,0:T(8,128)(2,1)S(1)} %fusion.95), channel_id=1, source_target_pairs={{0,8},{8,16},{16,24},{1,9},{9,17},{17,25},{2,10},{10,18},{18,26},{... | collective-permute-start | bytes 589832 | tf_op jit(solution)/shard_map/ppermute | solution.py:15
  171.7 6.2 %collective-permute-start.6 = (bf16[128,768]{1,0:T(8,128)(2,1)S(1)}, bf16[128,768]{1,0:T(8,128)(2,1)S(1)}, u32[]{:S(2)}, u32[]{:S(2)}) collective-permute-start(bf16[128,768]{1,0:T(8,128)(2,1)S(1)} %fusion.96), channel_id=1, source_target_pairs={{0,8},{8,16},{16,24},{1,9},{9,17},{17,25},{2,10},{10,18},{18,26},{... | collective-permute-start | bytes 589832 | tf_op jit(solution)/shard_map/ppermute | solution.py:15
  181.5 10.5 %collective-permute-start.7 = (bf16[128,768]{1,0:T(8,128)(2,1)S(1)}, bf16[128,768]{1,0:T(8,128)(2,1)S(1)}, u32[]{:S(2)}, u32[]{:S(2)}) collective-permute-start(bf16[128,768]{1,0:T(8,128)(2,1)S(1)} %fusion.97), channel_id=1, source_target_pairs={{0,8},{8,16},{16,24},{1,9},{9,17},{17,25},{2,10},{10,18},{18,26},{... | collective-permute-start | bytes 589832 | tf_op jit(solution)/shard_map/ppermute | solution.py:15
  189.0 6.0 %collective-permute-start.8 = (bf16[128,768]{1,0:T(8,128)(2,1)S(1)}, bf16[128,768]{1,0:T(8,128)(2,1)S(1)}, u32[]{:S(2)}, u32[]{:S(2)}) collective-permute-start(bf16[128,768]{1,0:T(8,128)(2,1)S(1)} %fusion.98), channel_id=1, source_target_pairs={{0,8},{8,16},{16,24},{1,9},{9,17},{17,25},{2,10},{10,18},{18,26},{... | collective-permute-start | bytes 589832 | tf_op jit(solution)/shard_map/ppermute | solution.py:15
  198.5 10.4 %collective-permute-start.9 = (bf16[128,768]{1,0:T(8,128)(2,1)S(1)}, bf16[128,768]{1,0:T(8,128)(2,1)S(1)}, u32[]{:S(2)}, u32[]{:S(2)}) collective-permute-start(bf16[128,768]{1,0:T(8,128)(2,1)S(1)} %fusion.99), channel_id=1, source_target_pairs={{0,8},{8,16},{16,24},{1,9},{9,17},{17,25},{2,10},{10,18},{18,26},{... | collective-permute-start | bytes 589832 | tf_op jit(solution)/shard_map/ppermute | solution.py:15
  206.1 6.0 %collective-permute-start.10 = (bf16[128,768]{1,0:T(8,128)(2,1)S(1)}, bf16[128,768]{1,0:T(8,128)(2,1)S(1)}, u32[]{:S(2)}, u32[]{:S(2)}) collective-permute-start(bf16[128,768]{1,0:T(8,128)(2,1)S(1)} %fusion.100), channel_id=1, source_target_pairs={{0,8},{8,16},{16,24},{1,9},{9,17},{17,25},{2,10},{10,18},{18,26},{... | collective-permute-start | bytes 589832 | tf_op jit(solution)/shard_map/ppermute | solution.py:15
  215.5 10.6 %collective-permute-start.11 = (bf16[128,768]{1,0:T(8,128)(2,1)S(1)}, bf16[128,768]{1,0:T(8,128)(2,1)S(1)}, u32[]{:S(2)}, u32[]{:S(2)}) collective-permute-start(bf16[128,768]{1,0:T(8,128)(2,1)S(1)} %fusion.101), channel_id=1, source_target_pairs={{0,8},{8,16},{16,24},{1,9},{9,17},{17,25},{2,10},{10,18},{18,26},{... | collective-permute-start | bytes 589832 | tf_op jit(solution)/shard_map/ppermute | solution.py:15
  223.3 6.0 %collective-permute-start.12 = (bf16[128,768]{1,0:T(8,128)(2,1)S(1)}, bf16[128,768]{1,0:T(8,128)(2,1)S(1)}, u32[]{:S(2)}, u32[]{:S(2)}) collective-permute-start(bf16[128,768]{1,0:T(8,128)(2,1)S(1)} %fusion.102), channel_id=1, source_target_pairs={{0,8},{8,16},{16,24},{1,9},{9,17},{17,25},{2,10},{10,18},{18,26},{... | collective-permute-start | bytes 589832 | tf_op jit(solution)/shard_map/ppermute | solution.py:15
  246.4 8.0 %collective-permute-start.15 = (bf16[128,768]{1,0:T(8,128)(2,1)S(1)}, bf16[128,768]{1,0:T(8,128)(2,1)S(1)}, u32[]{:S(2)}, u32[]{:S(2)}) collective-permute-start(bf16[128,768]{1,0:T(8,128)(2,1)S(1)} %get-tuple-element.107), channel_id=1, source_target_pairs={{8,0},{16,8},{24,16},{9,1},{17,9},{25,17},{10,2},{18,10},{26,18},{... | collective-permute-start | bytes 589832 | tf_op jit(solution)/shard_map/ppermute | solution.py:15
  258.8 8.5 %collective-permute-start.17 = (bf16[128,768]{1,0:T(8,128)(2,1)S(1)}, bf16[128,768]{1,0:T(8,128)(2,1)S(1)}, u32[]{:S(2)}, u32[]{:S(2)}) collective-permute-start(bf16[128,768]{1,0:T(8,128)(2,1)S(1)} %fusion.472), channel_id=1, source_target_pairs={{8,0},{16,8},{24,16},{9,1},{17,9},{25,17},{10,2},{18,10},{26,18},{... | collective-permute-start | bytes 589832 | tf_op jit(solution)/shard_map/ppermute | solution.py:15
  271.2 8.5 %collective-permute-start.19 = (bf16[128,768]{1,0:T(8,128)(2,1)S(1)}, bf16[128,768]{1,0:T(8,128)(2,1)S(1)}, u32[]{:S(2)}, u32[]{:S(2)}) collective-permute-start(bf16[128,768]{1,0:T(8,128)(2,1)S(1)} %fusion.476), channel_id=1, source_target_pairs={{8,0},{16,8},{24,16},{9,1},{17,9},{25,17},{10,2},{18,10},{26,18},{... | collective-permute-start | bytes 589832 | tf_op jit(solution)/shard_map/ppermute | solution.py:15
  283.6 8.5 %collective-permute-start.21 = (bf16[128,768]{1,0:T(8,128)(2,1)S(1)}, bf16[128,768]{1,0:T(8,128)(2,1)S(1)}, u32[]{:S(2)}, u32[]{:S(2)}) collective-permute-start(bf16[128,768]{1,0:T(8,128)(2,1)S(1)} %fusion.480), channel_id=1, source_target_pairs={{8,0},{16,8},{24,16},{9,1},{17,9},{25,17},{10,2},{18,10},{26,18},{... | collective-permute-start | bytes 589832 | tf_op jit(solution)/shard_map/ppermute | solution.py:15
  295.6 9.6 %copy-start.51 = (f32[768]{0:T(1024)S(1)}, f32[768]{0:T(1024)}, u32[]{:S(2)}) copy-start(f32[768]{0:T(1024)} %fusion.676) | copy-start | bytes 9220
  295.9 9.2 %collective-permute-start.23 = (bf16[128,768]{1,0:T(8,128)(2,1)S(1)}, bf16[128,768]{1,0:T(8,128)(2,1)S(1)}, u32[]{:S(2)}, u32[]{:S(2)}) collective-permute-start(bf16[128,768]{1,0:T(8,128)(2,1)S(1)} %fusion.484), channel_id=1, source_target_pairs={{8,0},{16,8},{24,16},{9,1},{17,9},{25,17},{10,2},{18,10},{26,18},{... | collective-permute-start | bytes 589832 | tf_op jit(solution)/shard_map/ppermute | solution.py:15
  305.2 13.9 %slice-start.2 = ((s8[7077888]{0:T(1024)(128)(4,1)}), s8[4194304]{0:T(1024)(128)(4,1)S(1)}, s32[]{:S(2)}) async-start(s8[7077888]{0:T(1024)(128)(4,1)} %bitcast.1036), calls=%async_computation.8 | async-start | bytes 8388608
  306.8 10.6 %copy-start.46 = (f32[768]{0:T(1024)S(1)}, f32[768]{0:T(1024)}, u32[]{:S(2)}) copy-start(f32[768]{0:T(1024)} %fusion.694) | copy-start | bytes 9220
  306.8 12.2 %slice-start.3 = ((s8[7077888]{0:T(1024)(128)(4,1)}), s8[2883584]{0:T(1024)(128)(4,1)S(1)}, s32[]{:S(2)}) async-start(s8[7077888]{0:T(1024)(128)(4,1)} %bitcast.1036), calls=%async_computation.9 | async-start | bytes 5767168
  309.0 8.4 %collective-permute-start.14 = (bf16[128,768]{1,0:T(8,128)(2,1)S(1)}, bf16[128,768]{1,0:T(8,128)(2,1)S(1)}, u32[]{:S(2)}, u32[]{:S(2)}) collective-permute-start(bf16[128,768]{1,0:T(8,128)(2,1)S(1)} %fusion.228), channel_id=1, source_target_pairs={{8,0},{16,8},{24,16},{9,1},{17,9},{25,17},{10,2},{18,10},{26,18},{... | collective-permute-start | bytes 589832 | tf_op jit(solution)/shard_map/ppermute | solution.py:15
  323.3 12.0 %copy-start.45 = (f32[768]{0:T(1024)S(1)}, f32[768]{0:T(1024)}, u32[]{:S(2)}) copy-start(f32[768]{0:T(1024)} %fusion.690) | copy-start | bytes 9220
  323.9 73.9 %collective-permute-start.25 = (bf16[128,768]{1,0:T(8,128)(2,1)S(1)}, bf16[128,768]{1,0:T(8,128)(2,1)S(1)}, u32[]{:S(2)}, u32[]{:S(2)}) collective-permute-start(bf16[128,768]{1,0:T(8,128)(2,1)S(1)} %get-tuple-element.104), channel_id=1, source_target_pairs={{8,0},{16,8},{24,16},{9,1},{17,9},{25,17},{10,2},{18,10},{26,18},{... | collective-permute-start | bytes 589832 | tf_op jit(solution)/shard_map/ppermute | solution.py:15
  325.2 10.1 %collective-permute-start.16 = (bf16[128,768]{1,0:T(8,128)(2,1)S(1)}, bf16[128,768]{1,0:T(8,128)(2,1)S(1)}, u32[]{:S(2)}, u32[]{:S(2)}) collective-permute-start(bf16[128,768]{1,0:T(8,128)(2,1)S(1)} %get-tuple-element.105), channel_id=1, source_target_pairs={{8,0},{16,8},{24,16},{9,1},{17,9},{25,17},{10,2},{18,10},{26,18},{... | collective-permute-start | bytes 589832 | tf_op jit(solution)/shard_map/ppermute | solution.py:15
  338.8 13.1 %copy-start.44 = (f32[768]{0:T(1024)S(1)}, f32[768]{0:T(1024)}, u32[]{:S(2)}) copy-start(f32[768]{0:T(1024)} %fusion.686) | copy-start | bytes 9220
  341.1 10.8 %collective-permute-start.18 = (bf16[128,768]{1,0:T(8,128)(2,1)S(1)}, bf16[128,768]{1,0:T(8,128)(2,1)S(1)}, u32[]{:S(2)}, u32[]{:S(2)}) collective-permute-start(bf16[128,768]{1,0:T(8,128)(2,1)S(1)} %fusion.474), channel_id=1, source_target_pairs={{8,0},{16,8},{24,16},{9,1},{17,9},{25,17},{10,2},{18,10},{26,18},{... | collective-permute-start | bytes 589832 | tf_op jit(solution)/shard_map/ppermute | solution.py:15
  355.3 11.4 %copy-start.43 = (f32[768]{0:T(1024)S(1)}, f32[768]{0:T(1024)}, u32[]{:S(2)}) copy-start(f32[768]{0:T(1024)} %fusion.682) | copy-start | bytes 9220
  357.5 9.3 %collective-permute-start.20 = (bf16[128,768]{1,0:T(8,128)(2,1)S(1)}, bf16[128,768]{1,0:T(8,128)(2,1)S(1)}, u32[]{:S(2)}, u32[]{:S(2)}) collective-permute-start(bf16[128,768]{1,0:T(8,128)(2,1)S(1)} %fusion.478), channel_id=1, source_target_pairs={{8,0},{16,8},{24,16},{9,1},{17,9},{25,17},{10,2},{18,10},{26,18},{... | collective-permute-start | bytes 589832 | tf_op jit(solution)/shard_map/ppermute | solution.py:15
  370.1 10.5 %copy-start.42 = (f32[768]{0:T(1024)S(1)}, f32[768]{0:T(1024)}, u32[]{:S(2)}) copy-start(f32[768]{0:T(1024)} %fusion.678) | copy-start | bytes 9220
  372.3 8.3 %collective-permute-start.22 = (bf16[128,768]{1,0:T(8,128)(2,1)S(1)}, bf16[128,768]{1,0:T(8,128)(2,1)S(1)}, u32[]{:S(2)}, u32[]{:S(2)}) collective-permute-start(bf16[128,768]{1,0:T(8,128)(2,1)S(1)} %fusion.482), channel_id=1, source_target_pairs={{8,0},{16,8},{24,16},{9,1},{17,9},{25,17},{10,2},{18,10},{26,18},{... | collective-permute-start | bytes 589832 | tf_op jit(solution)/shard_map/ppermute | solution.py:15
  384.0 10.4 %copy-start.41 = (f32[768]{0:T(1024)S(1)}, f32[768]{0:T(1024)}, u32[]{:S(2)}) copy-start(f32[768]{0:T(1024)} %fusion.674) | copy-start | bytes 9220
  386.1 8.3 %collective-permute-start.24 = (bf16[128,768]{1,0:T(8,128)(2,1)S(1)}, bf16[128,768]{1,0:T(8,128)(2,1)S(1)}, u32[]{:S(2)}, u32[]{:S(2)}) collective-permute-start(bf16[128,768]{1,0:T(8,128)(2,1)S(1)} %fusion.486), channel_id=1, source_target_pairs={{8,0},{16,8},{24,16},{9,1},{17,9},{25,17},{10,2},{18,10},{26,18},{... | collective-permute-start | bytes 589832 | tf_op jit(solution)/shard_map/ppermute | solution.py:15
  387.8 10.0 %copy-start.40 = (f32[768]{0:T(1024)S(1)}, f32[768]{0:T(1024)}, u32[]{:S(2)}) copy-start(f32[768]{0:T(1024)} %fusion.672) | copy-start | bytes 9220
  409.2 111.8 %reduce-scatter.5.cloned.1.call-start = ((), (), s32[]{:S(2)}) async-start(), calls=%async_computation.4 | async-start | bytes 5529600 | tf_op jit(solution)/shard_map/reduce_scatter | solution.py:184
  (73 other events, 307.0 us)
Sparse Core Ops, SparseCore 0:
  10.2 55.8 all-gather.3
  67.7 49.8 all-gather.5
  409.3 54.2 reduce-scatter.2
  465.7 55.1 reduce-scatter.4
